TPU v7x, 32 devices: a whole 2x2x4 slice. The times are simulated.
32 devices in a mesh: gz: 8 (over z, y), xy: 4 (over x, core).
Axes of the slice: x: 2, y: 2, z: 4, core: 2. Of those that a mesh axis runs over, the one named last changes fastest.
Arguments:
- image: float32 [64, 512, 512], P('gz', 'xy'), may hold values from -6 to 6
- offsets: int32 [4, 64, 4, 4], P(None, 'gz', 'xy'), may hold values from -6 to 6
- frac_index: int32 [4, 64, 4, 4], P(None, 'gz', 'xy'), may hold values from 0 to 15
- fractions: float32 [16, 3], replicated, may hold values from 0 to 1
Outputs:
- transported: float32 [64, 512, 512], P('gz', 'xy')
All inputs are finite; a program needn't handle non-finite values.
Results may differ from a plain program's by a relative error of at most 0.0003.
Values sent between devices are 32-bit elements; how exact they have to be, the bound alone decides.
A program may use at most 128 MiB of HBM per device.

v0:
```python
import jax
import jax.numpy as jnp
from jax import lax
from jax.sharding import PartitionSpec as P


def extended(cells, sides, width):
    for axis, dim in sides:
        count = lax.axis_size(axis)
        head = lax.slice_in_dim(cells, 0, width, axis=dim)
        tail = lax.slice_in_dim(cells, cells.shape[dim] - width, cells.shape[dim], axis=dim)
        cells = jnp.concatenate(
            [
                lax.ppermute(tail, axis, [(i, (i + 1) % count) for i in range(count)]),
                cells,
                lax.ppermute(head, axis, [((i + 1) % count, i) for i in range(count)]),
            ],
            axis=dim,
        )
    return cells


def cubic_weights(shares):
    return (
        -shares * (shares - 1.0) * (shares - 2.0) / 6.0,
        (shares + 1.0) * (shares - 1.0) * (shares - 2.0) / 2.0,
        -(shares + 1.0) * shares * (shares - 2.0) / 2.0,
        (shares + 1.0) * shares * (shares - 1.0) / 6.0,
    )


def column_steps(image, offsets, frac_index, fractions):
    step_count = offsets.shape[0]
    all_shifts, all_index = (
        lax.all_gather(offsets, "gz", axis=1, tiled=True),
        lax.all_gather(frac_index, "gz", axis=1, tiled=True),
    )
    standing = jnp.swapaxes(
        lax.all_to_all(image, "gz", split_axis=2, concat_axis=0, tiled=True), 1, 2
    )
    total_planes = standing.shape[0]
    width_y = standing.shape[1]
    width_x = standing.shape[2]
    column_block = lax.axis_index("gz") * width_y // width_x
    block_pick = (jnp.arange(all_shifts.shape[3], dtype=jnp.int32) == column_block).astype(
        jnp.int32
    )
    levels = jnp.arange(total_planes, dtype=jnp.int32)
    table_rows = jnp.arange(fractions.shape[0], dtype=jnp.int32)
    for step_index in range(step_count):
        shifts_now = jnp.sum(all_shifts[step_index, :, 0, :] * block_pick[None, :], axis=1)
        index_now = jnp.sum(all_index[step_index, :, 0, :] * block_pick[None, :], axis=1)
        onehot = (index_now[:, None] == table_rows[None, :]).astype(jnp.float32)
        picked = jnp.dot(onehot, fractions, precision=lax.Precision.HIGHEST)
        zweights = cubic_weights(1.0 - picked[:, 0])
        xweights = cubic_weights(1.0 - picked[:, 1])
        yweights = cubic_weights(1.0 - picked[:, 2])
        rimmed = extended(standing, (("gz", 1), ("xy", 2)), 2)
        merged = jnp.zeros(rimmed.shape, jnp.float32)
        for node in range(4):
            source = jnp.mod(levels - shifts_now - 2 + node, total_planes)
            merged = merged + zweights[node][:, None, None] * jnp.take(rimmed, source, axis=0)
        along_y = jnp.zeros((total_planes, width_y, width_x + 4), jnp.float32)
        for node in range(4):
            along_y = along_y + yweights[node][:, None, None] * merged[:, node : node + width_y, :]
        along_x = jnp.zeros((total_planes, width_y, width_x), jnp.float32)
        for node in range(4):
            along_x = along_x + xweights[node][:, None, None] * along_y[:, :, node : node + width_x]
        standing = along_x
    return lax.all_to_all(
        jnp.swapaxes(standing, 1, 2), "gz", split_axis=0, concat_axis=2, tiled=True
    )


def local(image, offsets, frac_index, fractions):
    return column_steps(image, offsets, frac_index, fractions)


def solution(mesh):
    in_specs = (P("gz", "xy", None), P(None, "gz", "xy", None), P(None, "gz", "xy", None), P())
    out_specs = P("gz", "xy", None)
    return jax.shard_map(local, mesh=mesh, in_specs=in_specs, out_specs=out_specs, check_vma=False)
```

profile of v0, /device:TPU:0, one launch (start us, length us, event | category | flops | bytes accessed | tf_op | source)
XLA Modules:
  0.0 443.4 jit_solution(4297421122283835696)
XLA Ops:
  0.0 2.9 copy.20
  2.9 7.3 %all-to-all-start = ((f32[8,128,512]{1,0,2:T(8,128)}), f32[8,128,512]{1,0,2:T(8,128)S(1)}, u32[]{:S(2)}, u32[]{:S(2)}) async-start(f32[8,128,512]{1,0,2:T(8,128)} %copy.20), calls=%async_computation | async-start | bytes 4194304 | tf_op jit(solution)/shard_map/all_to_all | solution.py:39
  10.5 68.2 %all_gather.6 = s32[4,64,1,4]{3,0,2,1:T(4,128)S(1)} all-gather(s32[4,8,1,4]{3,0,2,1:T(4,128)S(1)} %copy.11), channel_id=1, replica_groups=mesh['gz'=8,'xy'=4] {'gz'}, dimensions={1}, use_global_device_ids=true | all-gather | bytes 4608 | tf_op jit(solution)/shard_map/all_gather | solution.py:36
  78.7 30.5 %all_gather.7 = s32[4,64,1,4]{3,0,2,1:T(4,128)S(1)} all-gather(s32[4,8,1,4]{3,0,2,1:T(4,128)S(1)} %copy.13), channel_id=1, replica_groups=mesh['gz'=8,'xy'=4] {'gz'}, dimensions={1}, use_global_device_ids=true | all-gather | bytes 4608 | tf_op jit(solution)/shard_map/all_gather | solution.py:35
  115.2 2.8 copy.23
  118.0 8.1 %fusion.160 = (f32[64,2,128]{1,2,0:T(8,128)}, f32[64,2,128]{1,2,0:T(8,128)}) fusion(f32[64,64,128]{1,2,0:T(8,128)} %bitcast.517), kind=kLoop, calls=%fused_computation.473 | loop fusion | bytes 262144 | tf_op jit(solution)/shard_map/slice | solution.py:11
  126.0 2.8 copy.24
  128.9 2.8 copy.25
  131.8 4.7 %collective-permute-start.1 = (f32[64,2,128]{2,0,1:T(8,128)S(1)}, f32[64,2,128]{2,0,1:T(8,128)S(1)}, u32[]{:S(2)}, u32[]{:S(2)}) collective-permute-start(f32[64,2,128]{2,0,1:T(8,128)S(1)} %copy.25), channel_id=1, source_target_pairs={{4,0},{8,4},{12,8},{16,12},{20,16},{24,20},{28,24},{0,28},{5,1},{9... | collective-permute-start | bytes 196616 | tf_op jit(solution)/shard_map/ppermute | solution.py:16
  136.5 2.7 copy.26
  139.3 2.7 copy.27
  143.8 2.2 collective-permute-start.3
  148.0 3.9 pad_maximum_fusion
  151.9 5.2 %gather_fusion = f32[64,68,132]{1,2,0:T(8,128)} fusion(f32[64,68,132]{1,2,0:T(8,128)} %pad_maximum_fusion, s32[1024]{0:T(1024)S(1)} %get-tuple-element.145), kind=kCustom, calls=%fused_computation.clone | custom fusion | bytes 4595968 | tf_op jit(solution)/shard_map/jit(_take)/gather | solution.py:62
  157.1 5.1 %gather_fusion.1 = f32[64,68,132]{1,2,0:T(8,128)} fusion(f32[64,68,132]{1,2,0:T(8,128)} %pad_maximum_fusion, s32[1024]{0:T(1024)S(1)} %get-tuple-element.144), kind=kCustom, calls=%fused_computation.1.clone | custom fusion | bytes 4595968 | tf_op jit(solution)/shard_map/jit(_take)/gather | solution.py:62
  162.2 5.2 %gather_fusion.2 = f32[64,68,132]{1,2,0:T(8,128)} fusion(f32[64,68,132]{1,2,0:T(8,128)} %pad_maximum_fusion, s32[1024]{0:T(1024)S(1)} %get-tuple-element.143), kind=kCustom, calls=%fused_computation.2.clone | custom fusion | bytes 4595968 | tf_op jit(solution)/shard_map/jit(_take)/gather | solution.py:62
  167.4 5.2 %gather_fusion.3 = f32[64,68,132]{1,2,0:T(8,128)} fusion(f32[64,68,132]{1,2,0:T(8,128)} %pad_maximum_fusion, s32[1024]{0:T(1024)S(1)} %get-tuple-element.142), kind=kCustom, calls=%fused_computation.3.clone | custom fusion | bytes 4595968 | tf_op jit(solution)/shard_map/jit(_take)/gather | solution.py:62
  172.6 7.3 %fusion.21 = f32[64,68,132]{1,2,0:T(8,128)S(1)} fusion(f32[64,68,132]{1,2,0:T(8,128)} %gather_fusion.3, f32[64,68,132]{1,2,0:T(8,128)} %gather_fusion.2, f32[64,68,132]{1,2,0:T(8,128)} %gather_fusion.1, f32[64,68,132]{1,2,0:T(8,128)} %gather_fusion, f32[64]{0:T(128)S(1)} %get-tuple-element.114, f32[64]{0:T(128)S(1)} %get-tuple-element.115, ...), kind=kLoop, calls=%fused_computation.70 | loop fusion | flops 6319104 | bytes 11490560 | tf_op jit(solution)/shard_map/add | solution.py:62
  179.9 4.5 %fusion.9 = f32[64,64,132]{1,2,0:T(8,128)S(1)} fusion(f32[64,68,132]{1,2,0:T(8,128)S(1)} %fusion.21, f32[64]{0:T(128)S(1)} %get-tuple-element.111, f32[64]{0:T(128)S(1)} %get-tuple-element.112, f32[64]{0:T(128)S(1)} %get-tuple-element.110, f32[64]{0:T(128)S(1)} %get-tuple-element.117), kind=kLoop, calls=%fused_computation.38 | loop fusion | flops 3784704 | bytes 10814464 | tf_op jit(solution)/shard_map/add | solution.py:65
  184.4 2.2 fusion.34
  186.6 4.9 %fusion.159 = (f32[64,2,128]{1,2,0:T(8,128)}, f32[64,2,128]{1,2,0:T(8,128)}) fusion(f32[64,64,128]{1,2,0:T(8,128)S(1)} %fusion.34), kind=kLoop, calls=%fused_computation.472 | loop fusion | bytes 262144 | tf_op jit(solution)/shard_map/slice | solution.py:11
  191.4 2.8 copy.28
  194.3 2.8 copy.29
  197.2 4.7 %collective-permute-start.5 = (f32[64,2,128]{2,0,1:T(8,128)S(1)}, f32[64,2,128]{2,0,1:T(8,128)S(1)}, u32[]{:S(2)}, u32[]{:S(2)}) collective-permute-start(f32[64,2,128]{2,0,1:T(8,128)S(1)} %copy.29), channel_id=1, source_target_pairs={{4,0},{8,4},{12,8},{16,12},{20,16},{24,20},{28,24},{0,28},{5,1},{9... | collective-permute-start | bytes 196616 | tf_op jit(solution)/shard_map/ppermute | solution.py:16
  201.9 2.7 copy.30
  204.7 2.7 copy.31
  213.1 3.9 pad_maximum_fusion.1
  216.9 5.2 %gather_fusion.4 = f32[64,68,132]{1,2,0:T(8,128)} fusion(f32[64,68,132]{1,2,0:T(8,128)} %pad_maximum_fusion.1, s32[1024]{0:T(1024)S(1)} %get-tuple-element.149), kind=kCustom, calls=%fused_computation.4.clone | custom fusion | bytes 4595968 | tf_op jit(solution)/shard_map/jit(_take)/gather | solution.py:62
  222.1 5.1 %gather_fusion.5 = f32[64,68,132]{1,2,0:T(8,128)} fusion(f32[64,68,132]{1,2,0:T(8,128)} %pad_maximum_fusion.1, s32[1024]{0:T(1024)S(1)} %get-tuple-element.148), kind=kCustom, calls=%fused_computation.5.clone | custom fusion | bytes 4595968 | tf_op jit(solution)/shard_map/jit(_take)/gather | solution.py:62
  227.3 5.2 %gather_fusion.6 = f32[64,68,132]{1,2,0:T(8,128)} fusion(f32[64,68,132]{1,2,0:T(8,128)} %pad_maximum_fusion.1, s32[1024]{0:T(1024)S(1)} %get-tuple-element.147), kind=kCustom, calls=%fused_computation.6.clone | custom fusion | bytes 4595968 | tf_op jit(solution)/shard_map/jit(_take)/gather | solution.py:62
  232.5 5.2 %gather_fusion.7 = f32[64,68,132]{1,2,0:T(8,128)} fusion(f32[64,68,132]{1,2,0:T(8,128)} %pad_maximum_fusion.1, s32[1024]{0:T(1024)S(1)} %get-tuple-element.146), kind=kCustom, calls=%fused_computation.7.clone | custom fusion | bytes 4595968 | tf_op jit(solution)/shard_map/jit(_take)/gather | solution.py:62
  237.7 7.3 %fusion.18 = f32[64,68,132]{1,2,0:T(8,128)S(1)} fusion(f32[64,68,132]{1,2,0:T(8,128)} %gather_fusion.7, f32[64,68,132]{1,2,0:T(8,128)} %gather_fusion.6, f32[64,68,132]{1,2,0:T(8,128)} %gather_fusion.5, f32[64,68,132]{1,2,0:T(8,128)} %gather_fusion.4, f32[64]{0:T(128)S(1)} %get-tuple-element.102, f32[64]{0:T(128)S(1)} %get-tuple-element.103, ...), kind=kLoop, calls=%fused_computation.63 | loop fusion | flops 6319104 | bytes 11490560 | tf_op jit(solution)/shard_map/add | solution.py:62
  245.0 4.5 %fusion.6 = f32[64,64,132]{1,2,0:T(8,128)S(1)} fusion(f32[64,68,132]{1,2,0:T(8,128)S(1)} %fusion.18, f32[64]{0:T(128)S(1)} %get-tuple-element.99, f32[64]{0:T(128)S(1)} %get-tuple-element.100, f32[64]{0:T(128)S(1)} %get-tuple-element.98, f32[64]{0:T(128)S(1)} %get-tuple-element.105), kind=kLoop, calls=%fused_computation.31 | loop fusion | flops 3784704 | bytes 10814464 | tf_op jit(solution)/shard_map/add | solution.py:65
  249.4 2.2 fusion.31
  251.6 4.9 %fusion.158 = (f32[64,2,128]{1,2,0:T(8,128)}, f32[64,2,128]{1,2,0:T(8,128)}) fusion(f32[64,64,128]{1,2,0:T(8,128)S(1)} %fusion.31), kind=kLoop, calls=%fused_computation.471 | loop fusion | bytes 262144 | tf_op jit(solution)/shard_map/slice | solution.py:11
  256.5 2.8 copy.32
  259.4 2.8 copy.33
  262.3 4.7 %collective-permute-start.9 = (f32[64,2,128]{2,0,1:T(8,128)S(1)}, f32[64,2,128]{2,0,1:T(8,128)S(1)}, u32[]{:S(2)}, u32[]{:S(2)}) collective-permute-start(f32[64,2,128]{2,0,1:T(8,128)S(1)} %copy.33), channel_id=1, source_target_pairs={{4,0},{8,4},{12,8},{16,12},{20,16},{24,20},{28,24},{0,28},{5,1},{9... | collective-permute-start | bytes 196616 | tf_op jit(solution)/shard_map/ppermute | solution.py:16
  267.0 2.7 copy.34
  269.7 2.7 copy.35
  278.2 3.9 pad_maximum_fusion.2
  282.0 5.2 %gather_fusion.8 = f32[64,68,132]{1,2,0:T(8,128)} fusion(f32[64,68,132]{1,2,0:T(8,128)} %pad_maximum_fusion.2, s32[1024]{0:T(1024)S(1)} %get-tuple-element.153), kind=kCustom, calls=%fused_computation.8.clone | custom fusion | bytes 4595968 | tf_op jit(solution)/shard_map/jit(_take)/gather | solution.py:62
  287.2 5.1 %gather_fusion.9 = f32[64,68,132]{1,2,0:T(8,128)} fusion(f32[64,68,132]{1,2,0:T(8,128)} %pad_maximum_fusion.2, s32[1024]{0:T(1024)S(1)} %get-tuple-element.152), kind=kCustom, calls=%fused_computation.9.clone | custom fusion | bytes 4595968 | tf_op jit(solution)/shard_map/jit(_take)/gather | solution.py:62
  292.4 5.2 %gather_fusion.10 = f32[64,68,132]{1,2,0:T(8,128)} fusion(f32[64,68,132]{1,2,0:T(8,128)} %pad_maximum_fusion.2, s32[1024]{0:T(1024)S(1)} %get-tuple-element.151), kind=kCustom, calls=%fused_computation.10.clone | custom fusion | bytes 4595968 | tf_op jit(solution)/shard_map/jit(_take)/gather | solution.py:62
  297.6 5.2 %gather_fusion.11 = f32[64,68,132]{1,2,0:T(8,128)} fusion(f32[64,68,132]{1,2,0:T(8,128)} %pad_maximum_fusion.2, s32[1024]{0:T(1024)S(1)} %get-tuple-element.150), kind=kCustom, calls=%fused_computation.11.clone | custom fusion | bytes 4595968 | tf_op jit(solution)/shard_map/jit(_take)/gather | solution.py:62
  302.8 7.3 %fusion.15 = f32[64,68,132]{1,2,0:T(8,128)S(1)} fusion(f32[64,68,132]{1,2,0:T(8,128)} %gather_fusion.11, f32[64,68,132]{1,2,0:T(8,128)} %gather_fusion.10, f32[64,68,132]{1,2,0:T(8,128)} %gather_fusion.9, f32[64,68,132]{1,2,0:T(8,128)} %gather_fusion.8, f32[64]{0:T(128)S(1)} %get-tuple-element.90, f32[64]{0:T(128)S(1)} %get-tuple-element.91, ...), kind=kLoop, calls=%fused_computation.56 | loop fusion | flops 6319104 | bytes 11490560 | tf_op jit(solution)/shard_map/add | solution.py:62
  310.1 4.5 %fusion.3 = f32[64,64,132]{1,2,0:T(8,128)S(1)} fusion(f32[64,68,132]{1,2,0:T(8,128)S(1)} %fusion.15, f32[64]{0:T(128)S(1)} %get-tuple-element.87, f32[64]{0:T(128)S(1)} %get-tuple-element.88, f32[64]{0:T(128)S(1)} %get-tuple-element.86, f32[64]{0:T(128)S(1)} %get-tuple-element.93), kind=kLoop, calls=%fused_computation.24 | loop fusion | flops 3784704 | bytes 10814464 | tf_op jit(solution)/shard_map/add | solution.py:65
  314.5 2.2 fusion.28
  316.7 4.9 %fusion.157 = (f32[64,2,128]{1,2,0:T(8,128)}, f32[64,2,128]{1,2,0:T(8,128)}) fusion(f32[64,64,128]{1,2,0:T(8,128)S(1)} %fusion.28), kind=kLoop, calls=%fused_computation.470 | loop fusion | bytes 262144 | tf_op jit(solution)/shard_map/slice | solution.py:11
  321.6 2.8 copy.36
  324.5 2.8 copy.37
  327.4 4.7 %collective-permute-start.13 = (f32[64,2,128]{2,0,1:T(8,128)S(1)}, f32[64,2,128]{2,0,1:T(8,128)S(1)}, u32[]{:S(2)}, u32[]{:S(2)}) collective-permute-start(f32[64,2,128]{2,0,1:T(8,128)S(1)} %copy.37), channel_id=1, source_target_pairs={{4,0},{8,4},{12,8},{16,12},{20,16},{24,20},{28,24},{0,28},{5,1},{9... | collective-permute-start | bytes 196616 | tf_op jit(solution)/shard_map/ppermute | solution.py:16
  332.1 2.7 copy.38
  334.9 2.7 copy.39
  343.3 3.8 pad_maximum_fusion.3
  347.2 5.1 %gather_fusion.12 = f32[64,68,132]{1,2,0:T(8,128)} fusion(f32[64,68,132]{1,2,0:T(8,128)} %pad_maximum_fusion.3, s32[1024]{0:T(1024)S(1)} %get-tuple-element.157), kind=kCustom, calls=%fused_computation.12.clone | custom fusion | bytes 4595968 | tf_op jit(solution)/shard_map/jit(_take)/gather | solution.py:62
  352.3 5.2 %gather_fusion.13 = f32[64,68,132]{1,2,0:T(8,128)} fusion(f32[64,68,132]{1,2,0:T(8,128)} %pad_maximum_fusion.3, s32[1024]{0:T(1024)S(1)} %get-tuple-element.156), kind=kCustom, calls=%fused_computation.13.clone | custom fusion | bytes 4595968 | tf_op jit(solution)/shard_map/jit(_take)/gather | solution.py:62
  357.6 5.2 %gather_fusion.14 = f32[64,68,132]{1,2,0:T(8,128)} fusion(f32[64,68,132]{1,2,0:T(8,128)} %pad_maximum_fusion.3, s32[1024]{0:T(1024)S(1)} %get-tuple-element.155), kind=kCustom, calls=%fused_computation.14.clone | custom fusion | bytes 4595968 | tf_op jit(solution)/shard_map/jit(_take)/gather | solution.py:62
  362.8 5.2 %gather_fusion.15 = f32[64,68,132]{1,2,0:T(8,128)} fusion(f32[64,68,132]{1,2,0:T(8,128)} %pad_maximum_fusion.3, s32[1024]{0:T(1024)S(1)} %get-tuple-element.154), kind=kCustom, calls=%fused_computation.15.clone | custom fusion | bytes 4595968 | tf_op jit(solution)/shard_map/jit(_take)/gather | solution.py:62
  368.1 7.3 %fusion.12 = f32[64,68,132]{1,2,0:T(8,128)S(1)} fusion(f32[64,68,132]{1,2,0:T(8,128)} %gather_fusion.15, f32[64,68,132]{1,2,0:T(8,128)} %gather_fusion.14, f32[64,68,132]{1,2,0:T(8,128)} %gather_fusion.13, f32[64,68,132]{1,2,0:T(8,128)} %gather_fusion.12, f32[64]{0:T(128)S(1)} %copy-done.25, f32[64]{0:T(128)S(1)} %copy-done.26, f32[64]{0:T(128)S(1)} %copy-done.24, ...), kind=kLoop, calls=%fused_computation.49 | loop fusion | flops 6319104 | bytes 11490560 | tf_op jit(solution)/shard_map/add | solution.py:62
  375.4 4.5 %fusion = f32[64,64,132]{1,2,0:T(8,128)S(1)} fusion(f32[64,68,132]{1,2,0:T(8,128)S(1)} %fusion.12, f32[64]{0:T(128)S(1)} %copy-done.33, f32[64]{0:T(128)S(1)} %copy-done.34, f32[64]{0:T(128)S(1)} %copy-done.32, f32[64]{0:T(128)S(1)} %copy-done.35), kind=kLoop, calls=%fused_computation.17 | loop fusion | flops 3784704 | bytes 10814464 | tf_op jit(solution)/shard_map/add | solution.py:65
  380.0 3.6 fusion.25
  383.6 2.8 copy.40
  386.4 54.7 %all_to_all.36 = f32[64,128,64]{1,2,0:T(8,128)S(1)} all-to-all(f32[64,128,64]{1,2,0:T(8,128)S(1)} %copy.40), channel_id=1, replica_groups=mesh['gz'=8,'xy'=4] {'gz'}, dimensions={0} | all-to-all | bytes 4194304 | tf_op jit(solution)/shard_map/all_to_all | solution.py:70
  (141 shorter events, 29.6 us)
Async XLA Ops:
  0.0 109.7 %copy-start = (f32[16,3]{0,1:T(4,128)S(1)}, f32[16,3]{0,1:T(4,128)}, u32[]{:S(2)}) copy-start(f32[16,3]{0,1:T(4,128)} %param.9) | copy-start | bytes 580
  0.0 10.2 %copy-start.18 = (s32[4,8,1,4]{1,3,2,0:T(4,128)S(1)}, s32[4,8,1,4]{1,3,2,0:T(4,128)}, u32[]{:S(2)}) copy-start(s32[4,8,1,4]{1,3,2,0:T(4,128)} %param.8) | copy-start | bytes 1540
  0.0 10.4 %copy-start.19 = (s32[4,8,1,4]{1,3,2,0:T(4,128)S(1)}, s32[4,8,1,4]{1,3,2,0:T(4,128)}, u32[]{:S(2)}) copy-start(s32[4,8,1,4]{1,3,2,0:T(4,128)} %param.7) | copy-start | bytes 1540
  2.9 109.0 %all-to-all-start = ((f32[8,128,512]{1,0,2:T(8,128)}), f32[8,128,512]{1,0,2:T(8,128)S(1)}, u32[]{:S(2)}, u32[]{:S(2)}) async-start(f32[8,128,512]{1,0,2:T(8,128)} %copy.20), calls=%async_computation | async-start | bytes 4194304 | tf_op jit(solution)/shard_map/all_to_all | solution.py:39
  111.9 1.3 copy-start.17
  128.9 7.7 %collective-permute-start = (f32[64,2,128]{2,0,1:T(8,128)S(1)}, f32[64,2,128]{2,0,1:T(8,128)S(1)}, u32[]{:S(2)}, u32[]{:S(2)}) collective-permute-start(f32[64,2,128]{2,0,1:T(8,128)S(1)} %copy.24), channel_id=1, source_target_pairs={{0,4},{4,8},{8,12},{12,16},{16,20},{20,24},{24,28},{28,0},{1,5},{5... | collective-permute-start | bytes 196616 | tf_op jit(solution)/shard_map/ppermute | solution.py:14
  131.8 7.5 %collective-permute-start.1 = (f32[64,2,128]{2,0,1:T(8,128)S(1)}, f32[64,2,128]{2,0,1:T(8,128)S(1)}, u32[]{:S(2)}, u32[]{:S(2)}) collective-permute-start(f32[64,2,128]{2,0,1:T(8,128)S(1)} %copy.25), channel_id=1, source_target_pairs={{4,0},{8,4},{12,8},{16,12},{20,16},{24,20},{28,24},{0,28},{5,1},{9... | collective-permute-start | bytes 196616 | tf_op jit(solution)/shard_map/ppermute | solution.py:16
  141.9 6.1 %copy-start.2 = (f32[64,128,64]{2,1,0:T(8,128)S(1)}, f32[64,128,64]{2,1,0:T(8,128)}, u32[]{:S(2)}) copy-start(f32[64,128,64]{2,1,0:T(8,128)} %copy.23) | copy-start | bytes 6291460
  141.9 6.1 %copy-start.9 = (f32[64,2,128]{1,2,0:T(8,128)S(1)}, f32[64,2,128]{1,2,0:T(8,128)}, u32[]{:S(2)}) copy-start(f32[64,2,128]{1,2,0:T(8,128)} %copy.26) | copy-start | bytes 196612
  141.9 6.1 %copy-start.13 = (f32[64,2,128]{1,2,0:T(8,128)S(1)}, f32[64,2,128]{1,2,0:T(8,128)}, u32[]{:S(2)}) copy-start(f32[64,2,128]{1,2,0:T(8,128)} %copy.27) | copy-start | bytes 196612
  143.8 3.7 collective-permute-start.2
  143.8 4.1 collective-permute-start.3
  186.6 4.9 %copy-start.3 = (f32[64,64,128]{1,2,0:T(8,128)}, f32[64,64,128]{1,2,0:T(8,128)S(1)}, u32[]{:S(2)}) copy-start(f32[64,64,128]{1,2,0:T(8,128)S(1)} %fusion.34) | copy-start | bytes 6291460
  194.3 7.7 %collective-permute-start.4 = (f32[64,2,128]{2,0,1:T(8,128)S(1)}, f32[64,2,128]{2,0,1:T(8,128)S(1)}, u32[]{:S(2)}, u32[]{:S(2)}) collective-permute-start(f32[64,2,128]{2,0,1:T(8,128)S(1)} %copy.28), channel_id=1, source_target_pairs={{0,4},{4,8},{8,12},{12,16},{16,20},{20,24},{24,28},{28,0},{1,5},{5... | collective-permute-start | bytes 196616 | tf_op jit(solution)/shard_map/ppermute | solution.py:14
  197.2 7.5 %collective-permute-start.5 = (f32[64,2,128]{2,0,1:T(8,128)S(1)}, f32[64,2,128]{2,0,1:T(8,128)S(1)}, u32[]{:S(2)}, u32[]{:S(2)}) collective-permute-start(f32[64,2,128]{2,0,1:T(8,128)S(1)} %copy.29), channel_id=1, source_target_pairs={{4,0},{8,4},{12,8},{16,12},{20,16},{24,20},{28,24},{0,28},{5,1},{9... | collective-permute-start | bytes 196616 | tf_op jit(solution)/shard_map/ppermute | solution.py:16
  207.3 5.7 %copy-start.4 = (f32[64,64,128]{1,2,0:T(8,128)S(1)}, f32[64,64,128]{1,2,0:T(8,128)}, u32[]{:S(2)}) copy-start(f32[64,64,128]{1,2,0:T(8,128)} %copy-done.3) | copy-start | bytes 6291460
  207.3 5.7 %copy-start.10 = (f32[64,2,128]{1,2,0:T(8,128)S(1)}, f32[64,2,128]{1,2,0:T(8,128)}, u32[]{:S(2)}) copy-start(f32[64,2,128]{1,2,0:T(8,128)} %copy.30) | copy-start | bytes 196612
  207.3 5.7 %copy-start.14 = (f32[64,2,128]{1,2,0:T(8,128)S(1)}, f32[64,2,128]{1,2,0:T(8,128)}, u32[]{:S(2)}) copy-start(f32[64,2,128]{1,2,0:T(8,128)} %copy.31) | copy-start | bytes 196612
  209.2 3.7 collective-permute-start.6
  210.3 2.7 collective-permute-start.7
  251.6 4.9 %copy-start.5 = (f32[64,64,128]{1,2,0:T(8,128)}, f32[64,64,128]{1,2,0:T(8,128)S(1)}, u32[]{:S(2)}) copy-start(f32[64,64,128]{1,2,0:T(8,128)S(1)} %fusion.31) | copy-start | bytes 6291460
  259.3 7.7 %collective-permute-start.8 = (f32[64,2,128]{2,0,1:T(8,128)S(1)}, f32[64,2,128]{2,0,1:T(8,128)S(1)}, u32[]{:S(2)}, u32[]{:S(2)}) collective-permute-start(f32[64,2,128]{2,0,1:T(8,128)S(1)} %copy.32), channel_id=1, source_target_pairs={{0,4},{4,8},{8,12},{12,16},{16,20},{20,24},{24,28},{28,0},{1,5},{5... | collective-permute-start | bytes 196616 | tf_op jit(solution)/shard_map/ppermute | solution.py:14
  262.3 7.5 %collective-permute-start.9 = (f32[64,2,128]{2,0,1:T(8,128)S(1)}, f32[64,2,128]{2,0,1:T(8,128)S(1)}, u32[]{:S(2)}, u32[]{:S(2)}) collective-permute-start(f32[64,2,128]{2,0,1:T(8,128)S(1)} %copy.33), channel_id=1, source_target_pairs={{4,0},{8,4},{12,8},{16,12},{20,16},{24,20},{28,24},{0,28},{5,1},{9... | collective-permute-start | bytes 196616 | tf_op jit(solution)/shard_map/ppermute | solution.py:16
  272.4 5.8 %copy-start.6 = (f32[64,64,128]{1,2,0:T(8,128)S(1)}, f32[64,64,128]{1,2,0:T(8,128)}, u32[]{:S(2)}) copy-start(f32[64,64,128]{1,2,0:T(8,128)} %copy-done.5) | copy-start | bytes 6291460
  272.4 5.8 %copy-start.11 = (f32[64,2,128]{1,2,0:T(8,128)S(1)}, f32[64,2,128]{1,2,0:T(8,128)}, u32[]{:S(2)}) copy-start(f32[64,2,128]{1,2,0:T(8,128)} %copy.34) | copy-start | bytes 196612
  272.4 5.8 %copy-start.15 = (f32[64,2,128]{1,2,0:T(8,128)S(1)}, f32[64,2,128]{1,2,0:T(8,128)}, u32[]{:S(2)}) copy-start(f32[64,2,128]{1,2,0:T(8,128)} %copy.35) | copy-start | bytes 196612
  274.3 3.7 collective-permute-start.10
  275.4 2.8 collective-permute-start.11
  316.7 4.9 %copy-start.7 = (f32[64,64,128]{1,2,0:T(8,128)}, f32[64,64,128]{1,2,0:T(8,128)S(1)}, u32[]{:S(2)}) copy-start(f32[64,64,128]{1,2,0:T(8,128)S(1)} %fusion.28) | copy-start | bytes 6291460
  321.6 10.5 %copy-start.38 = (s32[64]{0:T(128)S(1)}, s32[64]{0:T(128)}, u32[]{:S(2)}) copy-start(s32[64]{0:T(128)} %get-tuple-element.15) | copy-start | bytes 772
  321.6 10.5 %copy-start.39 = (s32[64]{0:T(128)S(1)}, s32[64]{0:T(128)}, u32[]{:S(2)}) copy-start(s32[64]{0:T(128)} %get-tuple-element.119) | copy-start | bytes 772
  324.5 7.7 %collective-permute-start.12 = (f32[64,2,128]{2,0,1:T(8,128)S(1)}, f32[64,2,128]{2,0,1:T(8,128)S(1)}, u32[]{:S(2)}, u32[]{:S(2)}) collective-permute-start(f32[64,2,128]{2,0,1:T(8,128)S(1)} %copy.36), channel_id=1, source_target_pairs={{0,4},{4,8},{8,12},{12,16},{16,20},{20,24},{24,28},{28,0},{1,5},{5... | collective-permute-start | bytes 196616 | tf_op jit(solution)/shard_map/ppermute | solution.py:14
  327.4 7.5 %collective-permute-start.13 = (f32[64,2,128]{2,0,1:T(8,128)S(1)}, f32[64,2,128]{2,0,1:T(8,128)S(1)}, u32[]{:S(2)}, u32[]{:S(2)}) collective-permute-start(f32[64,2,128]{2,0,1:T(8,128)S(1)} %copy.37), channel_id=1, source_target_pairs={{4,0},{8,4},{12,8},{16,12},{20,16},{24,20},{28,24},{0,28},{5,1},{9... | collective-permute-start | bytes 196616 | tf_op jit(solution)/shard_map/ppermute | solution.py:16
  337.5 3.9 copy-start.36
  337.5 3.9 copy-start.37
  337.5 5.8 %copy-start.8 = (f32[64,64,128]{1,2,0:T(8,128)S(1)}, f32[64,64,128]{1,2,0:T(8,128)}, u32[]{:S(2)}) copy-start(f32[64,64,128]{1,2,0:T(8,128)} %copy-done.7) | copy-start | bytes 6291460
  337.5 5.8 %copy-start.12 = (f32[64,2,128]{1,2,0:T(8,128)S(1)}, f32[64,2,128]{1,2,0:T(8,128)}, u32[]{:S(2)}) copy-start(f32[64,2,128]{1,2,0:T(8,128)} %copy.38) | copy-start | bytes 196612
  337.5 5.8 %copy-start.16 = (f32[64,2,128]{1,2,0:T(8,128)S(1)}, f32[64,2,128]{1,2,0:T(8,128)}, u32[]{:S(2)}) copy-start(f32[64,2,128]{1,2,0:T(8,128)} %copy.39) | copy-start | bytes 196612
  339.4 3.7 collective-permute-start.14
  340.6 2.7 collective-permute-start.15
  362.8 5.2 %copy-start.20 = (pred[64]{0:T(512)(128)(4,1)S(1)}, pred[64]{0:T(512)(128)(4,1)}, u32[]{:S(2)}) copy-start(pred[64]{0:T(512)(128)(4,1)} %get-tuple-element.14) | copy-start | bytes 196
  362.8 5.2 %copy-start.21 = (pred[64]{0:T(512)(128)(4,1)S(1)}, pred[64]{0:T(512)(128)(4,1)}, u32[]{:S(2)}) copy-start(pred[64]{0:T(512)(128)(4,1)} %get-tuple-element.118) | copy-start | bytes 196
  362.8 5.2 %copy-start.22 = (pred[64]{0:T(512)(128)(4,1)S(1)}, pred[64]{0:T(512)(128)(4,1)}, u32[]{:S(2)}) copy-start(pred[64]{0:T(512)(128)(4,1)} %get-tuple-element.120) | copy-start | bytes 196
  362.8 5.2 %copy-start.23 = (pred[64]{0:T(512)(128)(4,1)S(1)}, pred[64]{0:T(512)(128)(4,1)}, u32[]{:S(2)}) copy-start(pred[64]{0:T(512)(128)(4,1)} %get-tuple-element.122) | copy-start | bytes 196
  362.8 5.2 %copy-start.24 = (f32[64]{0:T(128)S(1)}, f32[64]{0:T(128)}, u32[]{:S(2)}) copy-start(f32[64]{0:T(128)} %get-tuple-element.77) | copy-start | bytes 772
  362.8 5.2 %copy-start.25 = (f32[64]{0:T(128)S(1)}, f32[64]{0:T(128)}, u32[]{:S(2)}) copy-start(f32[64]{0:T(128)} %get-tuple-element.78) | copy-start | bytes 772
  362.8 5.2 %copy-start.26 = (f32[64]{0:T(128)S(1)}, f32[64]{0:T(128)}, u32[]{:S(2)}) copy-start(f32[64]{0:T(128)} %get-tuple-element.79) | copy-start | bytes 772
  362.8 5.2 %copy-start.27 = (f32[64]{0:T(128)S(1)}, f32[64]{0:T(128)}, u32[]{:S(2)}) copy-start(f32[64]{0:T(128)} %get-tuple-element.80) | copy-start | bytes 772
  368.1 7.3 %copy-start.32 = (f32[64]{0:T(128)S(1)}, f32[64]{0:T(128)}, u32[]{:S(2)}) copy-start(f32[64]{0:T(128)} %get-tuple-element.74) | copy-start | bytes 772
  368.1 7.3 %copy-start.33 = (f32[64]{0:T(128)S(1)}, f32[64]{0:T(128)}, u32[]{:S(2)}) copy-start(f32[64]{0:T(128)} %get-tuple-element.75) | copy-start | bytes 772
  368.1 7.3 %copy-start.34 = (f32[64]{0:T(128)S(1)}, f32[64]{0:T(128)}, u32[]{:S(2)}) copy-start(f32[64]{0:T(128)} %get-tuple-element.76) | copy-start | bytes 772
  368.1 7.3 %copy-start.35 = (f32[64]{0:T(128)S(1)}, f32[64]{0:T(128)}, u32[]{:S(2)}) copy-start(f32[64]{0:T(128)} %get-tuple-element.81) | copy-start | bytes 772
  375.4 4.5 %copy-start.28 = (f32[64]{0:T(128)S(1)}, f32[64]{0:T(128)}, u32[]{:S(2)}) copy-start(f32[64]{0:T(128)} %get-tuple-element.70) | copy-start | bytes 772
  375.4 4.5 %copy-start.29 = (f32[64]{0:T(128)S(1)}, f32[64]{0:T(128)}, u32[]{:S(2)}) copy-start(f32[64]{0:T(128)} %get-tuple-element.71) | copy-start | bytes 772
  375.4 4.5 %copy-start.30 = (f32[64]{0:T(128)S(1)}, f32[64]{0:T(128)}, u32[]{:S(2)}) copy-start(f32[64]{0:T(128)} %get-tuple-element.72) | copy-start | bytes 772
  375.4 4.5 %copy-start.31 = (f32[64]{0:T(128)S(1)}, f32[64]{0:T(128)}, u32[]{:S(2)}) copy-start(f32[64]{0:T(128)} %get-tuple-element.73) | copy-start | bytes 772
  386.4 56.7 %copy-start.1 = (f32[16,3]{0,1:T(4,128)S(1)}, f32[16,3]{0,1:T(4,128)}, u32[]{:S(2)}) copy-start(f32[16,3]{0,1:T(4,128)} %param.9) | copy-start | bytes 580
where the time goes:
time: 449 us; the launch traced here: 443 us
  local copies, waits for them, and re-layouts  164 us (37%)
  blocking collectives  153 us (34%)
  other arithmetic  81.6 us (18%)
  starting transfers between devices  34.7 us (8%)
  waiting for transfers between devices  7.61 us (2%)
    gather x16, local copies, waits for them, and re-layouts, column_steps(): jnp.take(rimmed, source, axis=0)  83.1 us
    all_gather x1, blocking collectives, column_steps(): lax.all_gather(frac_index, 'gz', axis=1, tiled=True)  68.2 us
    all_to_all x1, blocking collectives, column_steps(): lax.all_to_all(jnp.swapaxes(standing, 1, 2), 'gz', split_axis=0, concat_a...  54.7 us
    slice x8, local copies, waits for them, and re-layouts, extended(): lax.slice_in_dim(cells, cells.shape[dim] - width, cells.shape[dim], axis=...  34 us
    all_gather x1, blocking collectives, column_steps(): lax.all_gather(offsets, 'gz', axis=1, tiled=True)  30.5 us
    add x4, other arithmetic, column_steps(): merged + zweights[node][:, None, None] * jnp.take(rimmed, source, axis=0)  29 us
    ppermute x8, starting transfers between devices, extended(): lax.ppermute(head, axis, [((i + 1) % count, i) for i in range(count)])  23.7 us
    add x4, other arithmetic, column_steps(): along_y + yweights[node][:, None, None] * merged[:, node:node + width_y, :]  17.9 us
  transfers between devices with their start and end apart: 17, of which 8 were waited for; matrix products, arithmetic and copies ran while one was open for 6% of the time, Pallas kernels for 0%

commit v1 on v0

--- a/solution.py
+++ b/solution.py
@@ -2,6 +2,12 @@
 import jax.numpy as jnp
 from jax import lax
 from jax.sharding import PartitionSpec as P
+
+
+def all_parts(x, mesh_axis, dim):
+    terms = lax.all_gather(x, mesh_axis, axis=0, tiled=False)
+    full = jnp.concatenate(terms, axis=dim)
+    return full
 
 
 def extended(cells, sides, width):
@@ -33,7 +39,7 @@
     step_count = offsets.shape[0]
     all_shifts, all_index = (
         lax.all_gather(offsets, "gz", axis=1, tiled=True),
-        lax.all_gather(frac_index, "gz", axis=1, tiled=True),
+        all_parts(frac_index, "gz", 1),
     )
     standing = jnp.swapaxes(
         lax.all_to_all(image, "gz", split_axis=2, concat_axis=0, tiled=True), 1, 2

time: 449 us -> 449 us (level)
  no operation moved by 1% of the time
where the time goes in v1:
time: 449 us; the launch traced here: 444 us
  local copies, waits for them, and re-layouts  165 us (37%)
  blocking collectives  153 us (34%)
  other arithmetic  81.7 us (18%)
  starting transfers between devices  34.7 us (8%)
  waiting for transfers between devices  7.61 us (2%)
    gather x16, local copies, waits for them, and re-layouts, column_steps(): jnp.take(rimmed, source, axis=0)  83.1 us
    all_gather x1, blocking collectives, all_parts(): terms = lax.all_gather(x, mesh_axis, axis=0, tiled=False)  68.3 us
    all_to_all x1, blocking collectives, column_steps(): lax.all_to_all(jnp.swapaxes(standing, 1, 2), 'gz', split_axis=0, concat_a...  54.7 us
    slice x8, local copies, waits for them, and re-layouts, extended(): lax.slice_in_dim(cells, cells.shape[dim] - width, cells.shape[dim], axis=...  34 us
    all_gather x1, blocking collectives, column_steps(): lax.all_gather(offsets, 'gz', axis=1, tiled=True)  30.5 us
    add x4, other arithmetic, column_steps(): merged + zweights[node][:, None, None] * jnp.take(rimmed, source, axis=0)  29 us
    ppermute x8, starting transfers between devices, extended(): lax.ppermute(head, axis, [((i + 1) % count, i) for i in range(count)])  23.7 us
    add x4, other arithmetic, column_steps(): along_y + yweights[node][:, None, None] * merged[:, node:node + width_y, :]  17.9 us
  transfers between devices with their start and end apart: 17, of which 8 were waited for; matrix products, arithmetic and copies ran while one was open for 6% of the time, Pallas kernels for 0%

profile of v1, /device:TPU:0, one launch (start us, length us, event | category | flops | bytes accessed | tf_op | source)
XLA Modules:
  0.0 443.7 jit_solution(11436704829284578045)
XLA Ops:
  0.0 2.9 copy.15
  2.9 7.3 %all-to-all-start = ((f32[8,128,512]{1,0,2:T(8,128)}), f32[8,128,512]{1,0,2:T(8,128)S(1)}, u32[]{:S(2)}, u32[]{:S(2)}) async-start(f32[8,128,512]{1,0,2:T(8,128)} %copy.15), calls=%async_computation | async-start | bytes 4194304 | tf_op jit(solution)/shard_map/all_to_all | solution.py:45
  10.4 68.3 %all-gather = s32[32,8,1,4]{1,3,2,0:T(4,128)S(1)} all-gather(s32[4,8,1,4]{1,3,2,0:T(4,128)S(1)} %copy-done.19), channel_id=2, replica_groups=mesh['gz'=8,'xy'=4] {'gz'}, dimensions={0}, use_global_device_ids=true | all-gather | bytes 4608 | tf_op jit(solution)/shard_map/all_gather | solution.py:8
  79.1 30.5 %all_gather.11 = s32[4,64,1,4]{3,0,2,1:T(4,128)S(1)} all-gather(s32[4,8,1,4]{3,0,2,1:T(4,128)S(1)} %copy.11), channel_id=1, replica_groups=mesh['gz'=8,'xy'=4] {'gz'}, dimensions={1}, use_global_device_ids=true | all-gather | bytes 4608 | tf_op jit(solution)/shard_map/all_gather | solution.py:41
  115.4 2.8 copy.18
  118.2 8.1 %fusion.164 = (f32[64,2,128]{1,2,0:T(8,128)}, f32[64,2,128]{1,2,0:T(8,128)}) fusion(f32[64,64,128]{1,2,0:T(8,128)} %bitcast.508), kind=kLoop, calls=%fused_computation.477 | loop fusion | bytes 262144 | tf_op jit(solution)/shard_map/slice | solution.py:17
  126.3 2.8 copy.19
  129.2 2.8 copy.20
  132.0 4.7 %collective-permute-start.1 = (f32[64,2,128]{2,0,1:T(8,128)S(1)}, f32[64,2,128]{2,0,1:T(8,128)S(1)}, u32[]{:S(2)}, u32[]{:S(2)}) collective-permute-start(f32[64,2,128]{2,0,1:T(8,128)S(1)} %copy.20), channel_id=1, source_target_pairs={{4,0},{8,4},{12,8},{16,12},{20,16},{24,20},{28,24},{0,28},{5,1},{9... | collective-permute-start | bytes 196616 | tf_op jit(solution)/shard_map/ppermute | solution.py:22
  136.8 2.7 copy.21
  139.5 2.7 copy.22
  144.1 2.2 collective-permute-start.3
  148.3 3.9 pad_maximum_fusion
  152.1 5.2 %gather_fusion = f32[64,68,132]{1,2,0:T(8,128)} fusion(f32[64,68,132]{1,2,0:T(8,128)} %pad_maximum_fusion, s32[1024]{0:T(1024)S(1)} %get-tuple-element.141), kind=kCustom, calls=%fused_computation.clone | custom fusion | bytes 4595968 | tf_op jit(solution)/shard_map/jit(_take)/gather | solution.py:68
  157.3 5.1 %gather_fusion.1 = f32[64,68,132]{1,2,0:T(8,128)} fusion(f32[64,68,132]{1,2,0:T(8,128)} %pad_maximum_fusion, s32[1024]{0:T(1024)S(1)} %get-tuple-element.140), kind=kCustom, calls=%fused_computation.1.clone | custom fusion | bytes 4595968 | tf_op jit(solution)/shard_map/jit(_take)/gather | solution.py:68
  162.5 5.2 %gather_fusion.2 = f32[64,68,132]{1,2,0:T(8,128)} fusion(f32[64,68,132]{1,2,0:T(8,128)} %pad_maximum_fusion, s32[1024]{0:T(1024)S(1)} %get-tuple-element.139), kind=kCustom, calls=%fused_computation.2.clone | custom fusion | bytes 4595968 | tf_op jit(solution)/shard_map/jit(_take)/gather | solution.py:68
  167.7 5.2 %gather_fusion.3 = f32[64,68,132]{1,2,0:T(8,128)} fusion(f32[64,68,132]{1,2,0:T(8,128)} %pad_maximum_fusion, s32[1024]{0:T(1024)S(1)} %get-tuple-element.138), kind=kCustom, calls=%fused_computation.3.clone | custom fusion | bytes 4595968 | tf_op jit(solution)/shard_map/jit(_take)/gather | solution.py:68
  172.9 7.3 %fusion.21 = f32[64,68,132]{1,2,0:T(8,128)S(1)} fusion(f32[64,68,132]{1,2,0:T(8,128)} %gather_fusion.3, f32[64,68,132]{1,2,0:T(8,128)} %gather_fusion.2, f32[64,68,132]{1,2,0:T(8,128)} %gather_fusion.1, f32[64,68,132]{1,2,0:T(8,128)} %gather_fusion, f32[64]{0:T(128)S(1)} %get-tuple-element.110, f32[64]{0:T(128)S(1)} %get-tuple-element.111, ...), kind=kLoop, calls=%fused_computation.70 | loop fusion | flops 6319104 | bytes 11490560 | tf_op jit(solution)/shard_map/add | solution.py:68
  180.2 4.5 %fusion.9 = f32[64,64,132]{1,2,0:T(8,128)S(1)} fusion(f32[64,68,132]{1,2,0:T(8,128)S(1)} %fusion.21, f32[64]{0:T(128)S(1)} %get-tuple-element.107, f32[64]{0:T(128)S(1)} %get-tuple-element.108, f32[64]{0:T(128)S(1)} %get-tuple-element.106, f32[64]{0:T(128)S(1)} %get-tuple-element.113), kind=kLoop, calls=%fused_computation.38 | loop fusion | flops 3784704 | bytes 10814464 | tf_op jit(solution)/shard_map/add | solution.py:71
  184.6 2.2 fusion.34
  186.8 4.9 %fusion.163 = (f32[64,2,128]{1,2,0:T(8,128)}, f32[64,2,128]{1,2,0:T(8,128)}) fusion(f32[64,64,128]{1,2,0:T(8,128)S(1)} %fusion.34), kind=kLoop, calls=%fused_computation.476 | loop fusion | bytes 262144 | tf_op jit(solution)/shard_map/slice | solution.py:17
  191.7 2.8 copy.23
  194.6 2.8 copy.24
  197.4 4.7 %collective-permute-start.5 = (f32[64,2,128]{2,0,1:T(8,128)S(1)}, f32[64,2,128]{2,0,1:T(8,128)S(1)}, u32[]{:S(2)}, u32[]{:S(2)}) collective-permute-start(f32[64,2,128]{2,0,1:T(8,128)S(1)} %copy.24), channel_id=1, source_target_pairs={{4,0},{8,4},{12,8},{16,12},{20,16},{24,20},{28,24},{0,28},{5,1},{9... | collective-permute-start | bytes 196616 | tf_op jit(solution)/shard_map/ppermute | solution.py:22
  202.2 2.7 copy.25
  204.9 2.7 copy.26
  213.3 3.9 pad_maximum_fusion.1
  217.2 5.2 %gather_fusion.4 = f32[64,68,132]{1,2,0:T(8,128)} fusion(f32[64,68,132]{1,2,0:T(8,128)} %pad_maximum_fusion.1, s32[1024]{0:T(1024)S(1)} %get-tuple-element.145), kind=kCustom, calls=%fused_computation.4.clone | custom fusion | bytes 4595968 | tf_op jit(solution)/shard_map/jit(_take)/gather | solution.py:68
  222.4 5.1 %gather_fusion.5 = f32[64,68,132]{1,2,0:T(8,128)} fusion(f32[64,68,132]{1,2,0:T(8,128)} %pad_maximum_fusion.1, s32[1024]{0:T(1024)S(1)} %get-tuple-element.144), kind=kCustom, calls=%fused_computation.5.clone | custom fusion | bytes 4595968 | tf_op jit(solution)/shard_map/jit(_take)/gather | solution.py:68
  227.5 5.2 %gather_fusion.6 = f32[64,68,132]{1,2,0:T(8,128)} fusion(f32[64,68,132]{1,2,0:T(8,128)} %pad_maximum_fusion.1, s32[1024]{0:T(1024)S(1)} %get-tuple-element.143), kind=kCustom, calls=%fused_computation.6.clone | custom fusion | bytes 4595968 | tf_op jit(solution)/shard_map/jit(_take)/gather | solution.py:68
  232.8 5.2 %gather_fusion.7 = f32[64,68,132]{1,2,0:T(8,128)} fusion(f32[64,68,132]{1,2,0:T(8,128)} %pad_maximum_fusion.1, s32[1024]{0:T(1024)S(1)} %get-tuple-element.142), kind=kCustom, calls=%fused_computation.7.clone | custom fusion | bytes 4595968 | tf_op jit(solution)/shard_map/jit(_take)/gather | solution.py:68
  238.0 7.3 %fusion.18 = f32[64,68,132]{1,2,0:T(8,128)S(1)} fusion(f32[64,68,132]{1,2,0:T(8,128)} %gather_fusion.7, f32[64,68,132]{1,2,0:T(8,128)} %gather_fusion.6, f32[64,68,132]{1,2,0:T(8,128)} %gather_fusion.5, f32[64,68,132]{1,2,0:T(8,128)} %gather_fusion.4, f32[64]{0:T(128)S(1)} %get-tuple-element.98, f32[64]{0:T(128)S(1)} %get-tuple-element.99, ...), kind=kLoop, calls=%fused_computation.63 | loop fusion | flops 6319104 | bytes 11490560 | tf_op jit(solution)/shard_map/add | solution.py:68
  245.2 4.5 %fusion.6 = f32[64,64,132]{1,2,0:T(8,128)S(1)} fusion(f32[64,68,132]{1,2,0:T(8,128)S(1)} %fusion.18, f32[64]{0:T(128)S(1)} %get-tuple-element.95, f32[64]{0:T(128)S(1)} %get-tuple-element.96, f32[64]{0:T(128)S(1)} %get-tuple-element.94, f32[64]{0:T(128)S(1)} %get-tuple-element.101), kind=kLoop, calls=%fused_computation.31 | loop fusion | flops 3784704 | bytes 10814464 | tf_op jit(solution)/shard_map/add | solution.py:71
  249.7 2.2 fusion.31
  251.9 4.9 %fusion.162 = (f32[64,2,128]{1,2,0:T(8,128)}, f32[64,2,128]{1,2,0:T(8,128)}) fusion(f32[64,64,128]{1,2,0:T(8,128)S(1)} %fusion.31), kind=kLoop, calls=%fused_computation.475 | loop fusion | bytes 262144 | tf_op jit(solution)/shard_map/slice | solution.py:17
  256.8 2.8 copy.27
  259.7 2.8 copy.28
  262.5 4.7 %collective-permute-start.9 = (f32[64,2,128]{2,0,1:T(8,128)S(1)}, f32[64,2,128]{2,0,1:T(8,128)S(1)}, u32[]{:S(2)}, u32[]{:S(2)}) collective-permute-start(f32[64,2,128]{2,0,1:T(8,128)S(1)} %copy.28), channel_id=1, source_target_pairs={{4,0},{8,4},{12,8},{16,12},{20,16},{24,20},{28,24},{0,28},{5,1},{9... | collective-permute-start | bytes 196616 | tf_op jit(solution)/shard_map/ppermute | solution.py:22
  267.3 2.7 copy.29
  270.0 2.7 copy.30
  278.4 3.9 pad_maximum_fusion.2
  282.3 5.2 %gather_fusion.8 = f32[64,68,132]{1,2,0:T(8,128)} fusion(f32[64,68,132]{1,2,0:T(8,128)} %pad_maximum_fusion.2, s32[1024]{0:T(1024)S(1)} %get-tuple-element.149), kind=kCustom, calls=%fused_computation.8.clone | custom fusion | bytes 4595968 | tf_op jit(solution)/shard_map/jit(_take)/gather | solution.py:68
  287.5 5.1 %gather_fusion.9 = f32[64,68,132]{1,2,0:T(8,128)} fusion(f32[64,68,132]{1,2,0:T(8,128)} %pad_maximum_fusion.2, s32[1024]{0:T(1024)S(1)} %get-tuple-element.148), kind=kCustom, calls=%fused_computation.9.clone | custom fusion | bytes 4595968 | tf_op jit(solution)/shard_map/jit(_take)/gather | solution.py:68
  292.6 5.2 %gather_fusion.10 = f32[64,68,132]{1,2,0:T(8,128)} fusion(f32[64,68,132]{1,2,0:T(8,128)} %pad_maximum_fusion.2, s32[1024]{0:T(1024)S(1)} %get-tuple-element.147), kind=kCustom, calls=%fused_computation.10.clone | custom fusion | bytes 4595968 | tf_op jit(solution)/shard_map/jit(_take)/gather | solution.py:68
  297.9 5.2 %gather_fusion.11 = f32[64,68,132]{1,2,0:T(8,128)} fusion(f32[64,68,132]{1,2,0:T(8,128)} %pad_maximum_fusion.2, s32[1024]{0:T(1024)S(1)} %get-tuple-element.146), kind=kCustom, calls=%fused_computation.11.clone | custom fusion | bytes 4595968 | tf_op jit(solution)/shard_map/jit(_take)/gather | solution.py:68
  303.1 7.3 %fusion.15 = f32[64,68,132]{1,2,0:T(8,128)S(1)} fusion(f32[64,68,132]{1,2,0:T(8,128)} %gather_fusion.11, f32[64,68,132]{1,2,0:T(8,128)} %gather_fusion.10, f32[64,68,132]{1,2,0:T(8,128)} %gather_fusion.9, f32[64,68,132]{1,2,0:T(8,128)} %gather_fusion.8, f32[64]{0:T(128)S(1)} %get-tuple-element.86, f32[64]{0:T(128)S(1)} %get-tuple-element.87, ...), kind=kLoop, calls=%fused_computation.56 | loop fusion | flops 6319104 | bytes 11490560 | tf_op jit(solution)/shard_map/add | solution.py:68
  310.3 4.5 %fusion.3 = f32[64,64,132]{1,2,0:T(8,128)S(1)} fusion(f32[64,68,132]{1,2,0:T(8,128)S(1)} %fusion.15, f32[64]{0:T(128)S(1)} %get-tuple-element.83, f32[64]{0:T(128)S(1)} %get-tuple-element.84, f32[64]{0:T(128)S(1)} %get-tuple-element.82, f32[64]{0:T(128)S(1)} %get-tuple-element.89), kind=kLoop, calls=%fused_computation.24 | loop fusion | flops 3784704 | bytes 10814464 | tf_op jit(solution)/shard_map/add | solution.py:71
  314.8 2.2 fusion.28
  317.0 4.9 %fusion.161 = (f32[64,2,128]{1,2,0:T(8,128)}, f32[64,2,128]{1,2,0:T(8,128)}) fusion(f32[64,64,128]{1,2,0:T(8,128)S(1)} %fusion.28), kind=kLoop, calls=%fused_computation.474 | loop fusion | bytes 262144 | tf_op jit(solution)/shard_map/slice | solution.py:17
  321.9 2.8 copy.31
  324.8 2.8 copy.32
  327.6 4.7 %collective-permute-start.13 = (f32[64,2,128]{2,0,1:T(8,128)S(1)}, f32[64,2,128]{2,0,1:T(8,128)S(1)}, u32[]{:S(2)}, u32[]{:S(2)}) collective-permute-start(f32[64,2,128]{2,0,1:T(8,128)S(1)} %copy.32), channel_id=1, source_target_pairs={{4,0},{8,4},{12,8},{16,12},{20,16},{24,20},{28,24},{0,28},{5,1},{9... | collective-permute-start | bytes 196616 | tf_op jit(solution)/shard_map/ppermute | solution.py:22
  332.4 2.7 copy.33
  335.1 2.7 copy.34
  343.6 3.8 pad_maximum_fusion.3
  347.4 5.1 %gather_fusion.12 = f32[64,68,132]{1,2,0:T(8,128)} fusion(f32[64,68,132]{1,2,0:T(8,128)} %pad_maximum_fusion.3, s32[1024]{0:T(1024)S(1)} %get-tuple-element.153), kind=kCustom, calls=%fused_computation.12.clone | custom fusion | bytes 4595968 | tf_op jit(solution)/shard_map/jit(_take)/gather | solution.py:68
  352.6 5.2 %gather_fusion.13 = f32[64,68,132]{1,2,0:T(8,128)} fusion(f32[64,68,132]{1,2,0:T(8,128)} %pad_maximum_fusion.3, s32[1024]{0:T(1024)S(1)} %get-tuple-element.152), kind=kCustom, calls=%fused_computation.13.clone | custom fusion | bytes 4595968 | tf_op jit(solution)/shard_map/jit(_take)/gather | solution.py:68
  357.8 5.2 %gather_fusion.14 = f32[64,68,132]{1,2,0:T(8,128)} fusion(f32[64,68,132]{1,2,0:T(8,128)} %pad_maximum_fusion.3, s32[1024]{0:T(1024)S(1)} %get-tuple-element.151), kind=kCustom, calls=%fused_computation.14.clone | custom fusion | bytes 4595968 | tf_op jit(solution)/shard_map/jit(_take)/gather | solution.py:68
  363.1 5.2 %gather_fusion.15 = f32[64,68,132]{1,2,0:T(8,128)} fusion(f32[64,68,132]{1,2,0:T(8,128)} %pad_maximum_fusion.3, s32[1024]{0:T(1024)S(1)} %get-tuple-element.150), kind=kCustom, calls=%fused_computation.15.clone | custom fusion | bytes 4595968 | tf_op jit(solution)/shard_map/jit(_take)/gather | solution.py:68
  368.3 7.3 %fusion.12 = f32[64,68,132]{1,2,0:T(8,128)S(1)} fusion(f32[64,68,132]{1,2,0:T(8,128)} %gather_fusion.15, f32[64,68,132]{1,2,0:T(8,128)} %gather_fusion.14, f32[64,68,132]{1,2,0:T(8,128)} %gather_fusion.13, f32[64,68,132]{1,2,0:T(8,128)} %gather_fusion.12, f32[64]{0:T(128)S(1)} %copy-done.25, f32[64]{0:T(128)S(1)} %copy-done.26, f32[64]{0:T(128)S(1)} %copy-done.24, ...), kind=kLoop, calls=%fused_computation.49 | loop fusion | flops 6319104 | bytes 11490560 | tf_op jit(solution)/shard_map/add | solution.py:68
  375.7 4.5 %fusion = f32[64,64,132]{1,2,0:T(8,128)S(1)} fusion(f32[64,68,132]{1,2,0:T(8,128)S(1)} %fusion.12, f32[64]{0:T(128)S(1)} %copy-done.33, f32[64]{0:T(128)S(1)} %copy-done.34, f32[64]{0:T(128)S(1)} %copy-done.32, f32[64]{0:T(128)S(1)} %copy-done.35), kind=kLoop, calls=%fused_computation.17 | loop fusion | flops 3784704 | bytes 10814464 | tf_op jit(solution)/shard_map/add | solution.py:71
  380.2 3.6 fusion.25
  383.8 2.8 copy.35
  386.7 54.7 %all_to_all.36 = f32[64,128,64]{1,2,0:T(8,128)S(1)} all-to-all(f32[64,128,64]{1,2,0:T(8,128)S(1)} %copy.35), channel_id=1, replica_groups=mesh['gz'=8,'xy'=4] {'gz'}, dimensions={0} | all-to-all | bytes 4194304 | tf_op jit(solution)/shard_map/all_to_all | solution.py:76
  (144 shorter events, 29.8 us)
Async XLA Ops:
  0.0 109.9 %copy-start = (f32[16,3]{0,1:T(4,128)S(1)}, f32[16,3]{0,1:T(4,128)}, u32[]{:S(2)}) copy-start(f32[16,3]{0,1:T(4,128)} %param.9) | copy-start | bytes 580
  0.0 10.2 %copy-start.18 = (s32[4,8,1,4]{1,3,2,0:T(4,128)S(1)}, s32[4,8,1,4]{1,3,2,0:T(4,128)}, u32[]{:S(2)}) copy-start(s32[4,8,1,4]{1,3,2,0:T(4,128)} %param.7) | copy-start | bytes 1540
  0.0 10.4 %copy-start.19 = (s32[4,8,1,4]{1,3,2,0:T(4,128)S(1)}, s32[4,8,1,4]{1,3,2,0:T(4,128)}, u32[]{:S(2)}) copy-start(s32[4,8,1,4]{1,3,2,0:T(4,128)} %param.8) | copy-start | bytes 1540
  2.9 109.2 %all-to-all-start = ((f32[8,128,512]{1,0,2:T(8,128)}), f32[8,128,512]{1,0,2:T(8,128)S(1)}, u32[]{:S(2)}, u32[]{:S(2)}) async-start(f32[8,128,512]{1,0,2:T(8,128)} %copy.15), calls=%async_computation | async-start | bytes 4194304 | tf_op jit(solution)/shard_map/all_to_all | solution.py:45
  112.2 1.3 copy-start.17
  129.1 7.7 %collective-permute-start = (f32[64,2,128]{2,0,1:T(8,128)S(1)}, f32[64,2,128]{2,0,1:T(8,128)S(1)}, u32[]{:S(2)}, u32[]{:S(2)}) collective-permute-start(f32[64,2,128]{2,0,1:T(8,128)S(1)} %copy.19), channel_id=1, source_target_pairs={{0,4},{4,8},{8,12},{12,16},{16,20},{20,24},{24,28},{28,0},{1,5},{5... | collective-permute-start | bytes 196616 | tf_op jit(solution)/shard_map/ppermute | solution.py:20
  132.0 7.5 %collective-permute-start.1 = (f32[64,2,128]{2,0,1:T(8,128)S(1)}, f32[64,2,128]{2,0,1:T(8,128)S(1)}, u32[]{:S(2)}, u32[]{:S(2)}) collective-permute-start(f32[64,2,128]{2,0,1:T(8,128)S(1)} %copy.20), channel_id=1, source_target_pairs={{4,0},{8,4},{12,8},{16,12},{20,16},{24,20},{28,24},{0,28},{5,1},{9... | collective-permute-start | bytes 196616 | tf_op jit(solution)/shard_map/ppermute | solution.py:22
  142.2 6.1 %copy-start.2 = (f32[64,128,64]{2,1,0:T(8,128)S(1)}, f32[64,128,64]{2,1,0:T(8,128)}, u32[]{:S(2)}) copy-start(f32[64,128,64]{2,1,0:T(8,128)} %copy.18) | copy-start | bytes 6291460
  142.2 6.1 %copy-start.9 = (f32[64,2,128]{1,2,0:T(8,128)S(1)}, f32[64,2,128]{1,2,0:T(8,128)}, u32[]{:S(2)}) copy-start(f32[64,2,128]{1,2,0:T(8,128)} %copy.21) | copy-start | bytes 196612
  142.2 6.1 %copy-start.13 = (f32[64,2,128]{1,2,0:T(8,128)S(1)}, f32[64,2,128]{1,2,0:T(8,128)}, u32[]{:S(2)}) copy-start(f32[64,2,128]{1,2,0:T(8,128)} %copy.22) | copy-start | bytes 196612
  144.0 3.7 collective-permute-start.2
  144.1 4.1 collective-permute-start.3
  186.8 4.9 %copy-start.3 = (f32[64,64,128]{1,2,0:T(8,128)}, f32[64,64,128]{1,2,0:T(8,128)S(1)}, u32[]{:S(2)}) copy-start(f32[64,64,128]{1,2,0:T(8,128)S(1)} %fusion.34) | copy-start | bytes 6291460
  194.5 7.7 %collective-permute-start.4 = (f32[64,2,128]{2,0,1:T(8,128)S(1)}, f32[64,2,128]{2,0,1:T(8,128)S(1)}, u32[]{:S(2)}, u32[]{:S(2)}) collective-permute-start(f32[64,2,128]{2,0,1:T(8,128)S(1)} %copy.23), channel_id=1, source_target_pairs={{0,4},{4,8},{8,12},{12,16},{16,20},{20,24},{24,28},{28,0},{1,5},{5... | collective-permute-start | bytes 196616 | tf_op jit(solution)/shard_map/ppermute | solution.py:20
  197.4 7.5 %collective-permute-start.5 = (f32[64,2,128]{2,0,1:T(8,128)S(1)}, f32[64,2,128]{2,0,1:T(8,128)S(1)}, u32[]{:S(2)}, u32[]{:S(2)}) collective-permute-start(f32[64,2,128]{2,0,1:T(8,128)S(1)} %copy.24), channel_id=1, source_target_pairs={{4,0},{8,4},{12,8},{16,12},{20,16},{24,20},{28,24},{0,28},{5,1},{9... | collective-permute-start | bytes 196616 | tf_op jit(solution)/shard_map/ppermute | solution.py:22
  207.6 5.7 %copy-start.4 = (f32[64,64,128]{1,2,0:T(8,128)S(1)}, f32[64,64,128]{1,2,0:T(8,128)}, u32[]{:S(2)}) copy-start(f32[64,64,128]{1,2,0:T(8,128)} %copy-done.3) | copy-start | bytes 6291460
  207.6 5.7 %copy-start.10 = (f32[64,2,128]{1,2,0:T(8,128)S(1)}, f32[64,2,128]{1,2,0:T(8,128)}, u32[]{:S(2)}) copy-start(f32[64,2,128]{1,2,0:T(8,128)} %copy.25) | copy-start | bytes 196612
  207.6 5.7 %copy-start.14 = (f32[64,2,128]{1,2,0:T(8,128)S(1)}, f32[64,2,128]{1,2,0:T(8,128)}, u32[]{:S(2)}) copy-start(f32[64,2,128]{1,2,0:T(8,128)} %copy.26) | copy-start | bytes 196612
  209.5 3.7 collective-permute-start.6
  210.6 2.7 collective-permute-start.7
  251.9 4.9 %copy-start.5 = (f32[64,64,128]{1,2,0:T(8,128)}, f32[64,64,128]{1,2,0:T(8,128)S(1)}, u32[]{:S(2)}) copy-start(f32[64,64,128]{1,2,0:T(8,128)S(1)} %fusion.31) | copy-start | bytes 6291460
  259.6 7.7 %collective-permute-start.8 = (f32[64,2,128]{2,0,1:T(8,128)S(1)}, f32[64,2,128]{2,0,1:T(8,128)S(1)}, u32[]{:S(2)}, u32[]{:S(2)}) collective-permute-start(f32[64,2,128]{2,0,1:T(8,128)S(1)} %copy.27), channel_id=1, source_target_pairs={{0,4},{4,8},{8,12},{12,16},{16,20},{20,24},{24,28},{28,0},{1,5},{5... | collective-permute-start | bytes 196616 | tf_op jit(solution)/shard_map/ppermute | solution.py:20
  262.5 7.5 %collective-permute-start.9 = (f32[64,2,128]{2,0,1:T(8,128)S(1)}, f32[64,2,128]{2,0,1:T(8,128)S(1)}, u32[]{:S(2)}, u32[]{:S(2)}) collective-permute-start(f32[64,2,128]{2,0,1:T(8,128)S(1)} %copy.28), channel_id=1, source_target_pairs={{4,0},{8,4},{12,8},{16,12},{20,16},{24,20},{28,24},{0,28},{5,1},{9... | collective-permute-start | bytes 196616 | tf_op jit(solution)/shard_map/ppermute | solution.py:22
  272.7 5.8 %copy-start.6 = (f32[64,64,128]{1,2,0:T(8,128)S(1)}, f32[64,64,128]{1,2,0:T(8,128)}, u32[]{:S(2)}) copy-start(f32[64,64,128]{1,2,0:T(8,128)} %copy-done.5) | copy-start | bytes 6291460
  272.7 5.8 %copy-start.11 = (f32[64,2,128]{1,2,0:T(8,128)S(1)}, f32[64,2,128]{1,2,0:T(8,128)}, u32[]{:S(2)}) copy-start(f32[64,2,128]{1,2,0:T(8,128)} %copy.29) | copy-start | bytes 196612
  272.7 5.8 %copy-start.15 = (f32[64,2,128]{1,2,0:T(8,128)S(1)}, f32[64,2,128]{1,2,0:T(8,128)}, u32[]{:S(2)}) copy-start(f32[64,2,128]{1,2,0:T(8,128)} %copy.30) | copy-start | bytes 196612
  274.5 3.7 collective-permute-start.10
  275.7 2.8 collective-permute-start.11
  317.0 4.9 %copy-start.7 = (f32[64,64,128]{1,2,0:T(8,128)}, f32[64,64,128]{1,2,0:T(8,128)S(1)}, u32[]{:S(2)}) copy-start(f32[64,64,128]{1,2,0:T(8,128)S(1)} %fusion.28) | copy-start | bytes 6291460
  321.9 10.5 %copy-start.38 = (s32[64]{0:T(128)S(1)}, s32[64]{0:T(128)}, u32[]{:S(2)}) copy-start(s32[64]{0:T(128)} %get-tuple-element.15) | copy-start | bytes 772
  321.9 10.5 %copy-start.39 = (s32[64]{0:T(128)S(1)}, s32[64]{0:T(128)}, u32[]{:S(2)}) copy-start(s32[64]{0:T(128)} %get-tuple-element.115) | copy-start | bytes 772
  324.7 7.7 %collective-permute-start.12 = (f32[64,2,128]{2,0,1:T(8,128)S(1)}, f32[64,2,128]{2,0,1:T(8,128)S(1)}, u32[]{:S(2)}, u32[]{:S(2)}) collective-permute-start(f32[64,2,128]{2,0,1:T(8,128)S(1)} %copy.31), channel_id=1, source_target_pairs={{0,4},{4,8},{8,12},{12,16},{16,20},{20,24},{24,28},{28,0},{1,5},{5... | collective-permute-start | bytes 196616 | tf_op jit(solution)/shard_map/ppermute | solution.py:20
  327.6 7.5 %collective-permute-start.13 = (f32[64,2,128]{2,0,1:T(8,128)S(1)}, f32[64,2,128]{2,0,1:T(8,128)S(1)}, u32[]{:S(2)}, u32[]{:S(2)}) collective-permute-start(f32[64,2,128]{2,0,1:T(8,128)S(1)} %copy.32), channel_id=1, source_target_pairs={{4,0},{8,4},{12,8},{16,12},{20,16},{24,20},{28,24},{0,28},{5,1},{9... | collective-permute-start | bytes 196616 | tf_op jit(solution)/shard_map/ppermute | solution.py:22
  337.8 3.9 copy-start.36
  337.8 3.9 copy-start.37
  337.8 5.8 %copy-start.8 = (f32[64,64,128]{1,2,0:T(8,128)S(1)}, f32[64,64,128]{1,2,0:T(8,128)}, u32[]{:S(2)}) copy-start(f32[64,64,128]{1,2,0:T(8,128)} %copy-done.7) | copy-start | bytes 6291460
  337.8 5.8 %copy-start.12 = (f32[64,2,128]{1,2,0:T(8,128)S(1)}, f32[64,2,128]{1,2,0:T(8,128)}, u32[]{:S(2)}) copy-start(f32[64,2,128]{1,2,0:T(8,128)} %copy.33) | copy-start | bytes 196612
  337.8 5.8 %copy-start.16 = (f32[64,2,128]{1,2,0:T(8,128)S(1)}, f32[64,2,128]{1,2,0:T(8,128)}, u32[]{:S(2)}) copy-start(f32[64,2,128]{1,2,0:T(8,128)} %copy.34) | copy-start | bytes 196612
  339.7 3.7 collective-permute-start.14
  340.9 2.7 collective-permute-start.15
  363.0 5.2 %copy-start.20 = (pred[64]{0:T(512)(128)(4,1)S(1)}, pred[64]{0:T(512)(128)(4,1)}, u32[]{:S(2)}) copy-start(pred[64]{0:T(512)(128)(4,1)} %get-tuple-element.14) | copy-start | bytes 196
  363.0 5.2 %copy-start.21 = (pred[64]{0:T(512)(128)(4,1)S(1)}, pred[64]{0:T(512)(128)(4,1)}, u32[]{:S(2)}) copy-start(pred[64]{0:T(512)(128)(4,1)} %get-tuple-element.114) | copy-start | bytes 196
  363.0 5.2 %copy-start.22 = (pred[64]{0:T(512)(128)(4,1)S(1)}, pred[64]{0:T(512)(128)(4,1)}, u32[]{:S(2)}) copy-start(pred[64]{0:T(512)(128)(4,1)} %get-tuple-element.116) | copy-start | bytes 196
  363.0 5.2 %copy-start.23 = (pred[64]{0:T(512)(128)(4,1)S(1)}, pred[64]{0:T(512)(128)(4,1)}, u32[]{:S(2)}) copy-start(pred[64]{0:T(512)(128)(4,1)} %get-tuple-element.118) | copy-start | bytes 196
  363.0 5.2 %copy-start.24 = (f32[64]{0:T(128)S(1)}, f32[64]{0:T(128)}, u32[]{:S(2)}) copy-start(f32[64]{0:T(128)} %get-tuple-element.73) | copy-start | bytes 772
  363.1 5.2 %copy-start.25 = (f32[64]{0:T(128)S(1)}, f32[64]{0:T(128)}, u32[]{:S(2)}) copy-start(f32[64]{0:T(128)} %get-tuple-element.74) | copy-start | bytes 772
  363.1 5.2 %copy-start.26 = (f32[64]{0:T(128)S(1)}, f32[64]{0:T(128)}, u32[]{:S(2)}) copy-start(f32[64]{0:T(128)} %get-tuple-element.75) | copy-start | bytes 772
  363.1 5.2 %copy-start.27 = (f32[64]{0:T(128)S(1)}, f32[64]{0:T(128)}, u32[]{:S(2)}) copy-start(f32[64]{0:T(128)} %get-tuple-element.76) | copy-start | bytes 772
  368.3 7.3 %copy-start.32 = (f32[64]{0:T(128)S(1)}, f32[64]{0:T(128)}, u32[]{:S(2)}) copy-start(f32[64]{0:T(128)} %get-tuple-element.70) | copy-start | bytes 772
  368.3 7.3 %copy-start.33 = (f32[64]{0:T(128)S(1)}, f32[64]{0:T(128)}, u32[]{:S(2)}) copy-start(f32[64]{0:T(128)} %get-tuple-element.71) | copy-start | bytes 772
  368.3 7.3 %copy-start.34 = (f32[64]{0:T(128)S(1)}, f32[64]{0:T(128)}, u32[]{:S(2)}) copy-start(f32[64]{0:T(128)} %get-tuple-element.72) | copy-start | bytes 772
  368.3 7.3 %copy-start.35 = (f32[64]{0:T(128)S(1)}, f32[64]{0:T(128)}, u32[]{:S(2)}) copy-start(f32[64]{0:T(128)} %get-tuple-element.77) | copy-start | bytes 772
  375.7 4.5 %copy-start.28 = (f32[64]{0:T(128)S(1)}, f32[64]{0:T(128)}, u32[]{:S(2)}) copy-start(f32[64]{0:T(128)} %get-tuple-element.66) | copy-start | bytes 772
  375.7 4.5 %copy-start.29 = (f32[64]{0:T(128)S(1)}, f32[64]{0:T(128)}, u32[]{:S(2)}) copy-start(f32[64]{0:T(128)} %get-tuple-element.67) | copy-start | bytes 772
  375.7 4.5 %copy-start.30 = (f32[64]{0:T(128)S(1)}, f32[64]{0:T(128)}, u32[]{:S(2)}) copy-start(f32[64]{0:T(128)} %get-tuple-element.68) | copy-start | bytes 772
  375.7 4.5 %copy-start.31 = (f32[64]{0:T(128)S(1)}, f32[64]{0:T(128)}, u32[]{:S(2)}) copy-start(f32[64]{0:T(128)} %get-tuple-element.69) | copy-start | bytes 772
  386.7 56.7 %copy-start.1 = (f32[16,3]{0,1:T(4,128)S(1)}, f32[16,3]{0,1:T(4,128)}, u32[]{:S(2)}) copy-start(f32[16,3]{0,1:T(4,128)} %param.9) | copy-start | bytes 580
